TPU v7x, 256 devices: a whole 4x4x8 slice. The times are simulated.
256 devices in a mesh: row: 32 (over z_hi, x, core), col: 8 (over y, z_lo).
Axes of the slice: x: 4, y: 4, z: 8 (z_hi: 4, z_lo: 2; z = z_hi * 2 + z_lo), core: 2. Of those that a mesh axis runs over, the one named last changes fastest.
Arguments:
- pivots: int32 [256], replicated, may hold values from 0 to 32767, as said below
- panel: float32 [32768, 256], P(('row', 'col')), may hold values from -6 to 6
- prior: bfloat16 [32768, 3072], P(('row', 'col')), may hold values from -0.796875 to 0.796875
- finished: bfloat16 [32768, 256], P(('row', 'col')), may hold values from -6 to 6
- pairs: int32 [32768], replicated, may hold values from 0 to 639999, as said below
- occupied: bfloat16 [800, 120], replicated, may hold values from -0.21875 to 0.21875
Outputs:
- updated: float32 [32768, 256], P(('row', 'col'))
- halves: float32 [256, 120, 800], P(('row', 'col'))
Inputs may be any that keep to these rules, and one draw needn't show every extreme that they name: `pivots`: distinct rows; at most 2 of them lie among the rows of one device (aligned blocks of 128 rows), and one device holds exactly 2. `pairs`: each value a * 800 + b with 0 <= b <= a < 800; all distinct and increasing.
All inputs are finite; a program needn't handle non-finite values.
Results may differ from a plain program's by a relative error of at most 0.0003.
Values may be sent and summed in bfloat16 or wider, within the bound.
A program may use at most 64 MiB of HBM per device.

v0:
```python
import jax
import jax.numpy as jnp
from jax import lax
from jax.sharding import PartitionSpec as P


def half_transform(received, pair_ids, occupied):
    orbitals = occupied.shape[0]
    pair_count = received.shape[0]
    vector_count = received.shape[1]
    first_ao = pair_ids // orbitals
    second_ao = pair_ids % orbitals
    off_diag = first_ao != second_ao
    occ_first = jnp.take(occupied, first_ao, axis=0)
    occ_second = jnp.where(
        off_diag[:, None], jnp.take(occupied, second_ao, axis=0), jnp.zeros((), jnp.bfloat16)
    )
    coeffs = jnp.concatenate([occ_first, occ_second], axis=0)
    targets = jnp.concatenate([second_ao, first_ao], axis=0).astype(jnp.int32)
    entries = jnp.concatenate([received, received], axis=0)
    doubled = 2 * pair_count
    wanted = min(doubled, max(1024, doubled // 8))
    block_rows = wanted
    for candidate in range(wanted, 0, -1):
        if doubled % candidate == 0:
            block_rows = candidate
            break
    columns = jnp.arange(orbitals, dtype=jnp.int32)

    def one_block(block_index, accumulated):
        start = block_index * block_rows
        coeff_block = lax.dynamic_slice_in_dim(coeffs, start, block_rows, 0)
        target_block = lax.dynamic_slice_in_dim(targets, start, block_rows, 0)
        entry_block = lax.dynamic_slice_in_dim(entries, start, block_rows, 0)
        matches = target_block[:, None] == columns[None, :]
        spread = jnp.where(
            matches[None, :, :], entry_block.T[:, :, None], jnp.zeros((), jnp.bfloat16)
        )
        return accumulated + jnp.einsum(
            "pi,vpm->vim", coeff_block, spread, preferred_element_type=jnp.float32
        )

    initial = jnp.zeros((vector_count, occupied.shape[1], orbitals), jnp.float32)
    return lax.fori_loop(0, doubled // block_rows, one_block, initial)


def per_device(pivots, panel, prior, finished, pairs, occupied):
    rows_dev = prior.shape[0]
    row_count = lax.axis_size("row")
    col_count = lax.axis_size("col")
    own_index = lax.axis_index("row") * col_count + lax.axis_index("col")
    owner = pivots // rows_dev
    local_rows = pivots % rows_dev
    owned = owner == own_index
    picked = jnp.take(prior, local_rows, axis=0).astype(jnp.float32)
    contribution = jnp.where(owned[:, None], picked, jnp.zeros_like(picked))
    pivot_rows = lax.psum(contribution, ("row", "col")).astype(jnp.bfloat16)
    updated = panel - lax.dot_general(
        prior, pivot_rows, (((1,), (1,)), ((), ())), preferred_element_type=jnp.float32
    )
    by_device = pairs.reshape(row_count, col_count, rows_dev)
    col_pairs = lax.dynamic_slice_in_dim(by_device, lax.axis_index("col"), 1, 1).reshape(-1)
    grouped = finished.reshape(rows_dev, row_count, finished.shape[1] // row_count)
    received = lax.all_to_all(grouped, "row", split_axis=1, concat_axis=0, tiled=True)
    partials = half_transform(
        received.reshape(received.shape[0], received.shape[2]), col_pairs, occupied
    )
    halves = lax.psum_scatter(partials, "col", scatter_dimension=0, tiled=True)
    return (updated, halves)


def solution(mesh):
    return jax.shard_map(
        per_device,
        mesh=mesh,
        in_specs=(
            P(),
            P(("row", "col"), None),
            P(("row", "col"), None),
            P(("row", "col"), None),
            P(),
            P(),
        ),
        out_specs=(P(("row", "col"), None), P(("row", "col"), None, None)),
        check_vma=False,
    )
```

profile of v0, /device:TPU:32, one launch (start us, length us, event | category | flops | bytes accessed | tf_op | source)
XLA Modules:
  0.0 254.6 jit_solution(17810283203826027613)
XLA Ops:
  7.2 0.0 copy-start
  7.2 0.0 copy-start.1
  7.2 1.7 copy.17
  8.9 10.4 %all-to-all-start = ((bf16[128,32,8]{0,2,1:T(8,128)(2,1)}), bf16[128,32,8]{0,2,1:T(8,128)(2,1)S(1)}, u32[]{:S(2)}, u32[]{:S(2)}) async-start(bf16[128,32,8]{0,2,1:T(8,128)(2,1)} %bitcast.4), calls=%async_computation | async-start | bytes 131072 | tf_op jit(solution)/shard_map/all_to_all | solution.py:64
  19.3 0.0 reduce-scatter.2.cloned.1.call-start
  19.3 1.0 broadcast_remainder_fusion
  20.3 1.0 compare_reduce_fusion
  21.4 0.0 copy-done.1
  21.4 12.1 %gather_fusion.2 = bf16[4096,120]{1,0:T(8,128)(2,1)S(1)} fusion(bf16[800,120]{1,0:T(8,128)(2,1)S(1)} %copy-done.1, s32[4096]{0:T(1024)S(1)} %get-tuple-element.172), kind=kCustom, calls=%fused_computation.1.clone | custom fusion | bytes 1982464 | tf_op jit(solution)/shard_map/jit(_take)/gather | solution.py:16
  33.5 12.1 %gather_fusion.1 = bf16[4096,120]{1,0:T(8,128)(2,1)S(1)} fusion(bf16[800,120]{1,0:T(8,128)(2,1)S(1)} %copy-done.1, s32[4096]{0:T(1024)S(1)} %fusion.21), kind=kCustom, calls=%fused_computation.clone | custom fusion | bytes 1982464 | tf_op jit(solution)/shard_map/jit(_take)/gather | solution.py:14
  45.7 2.1 broadcast_select_fusion
  47.8 1.4 select_select_fusion
  49.2 0.4 pad_maximum_fusion
  49.7 3.0 %copy.18 = bf16[8192,120]{0,1:T(8,128)(2,1)} copy(bf16[8192,120]{1,0:T(8,128)(2,1)S(1)} %pad_maximum_fusion) | data formatting | bytes 3932160
  52.6 0.0 all-to-all-done
  52.7 55.6 %while.14 = (s32[]{:T(128)}, f32[8,120,800]{1,2,0:T(8,128)}, s32[8192]{0:T(1024)S(1)}, bf16[8192,8]{0,1:T(8,128)(2,1)S(1)}, bf16[8192,120]{0,1:T(8,128)(2,1)}, /*index=5*/s32[]{:T(128)}, s32[]{:T(128)}, s32[]{:T(128)}, s32[]{:T(128)}) while((s32[]{:T(128)}, f32[8,120,800]{1,2,0:T(8,128)}, s32[8192]{0:T(1024)S(1)}, ...), condition=%wide.region_2.4_spmd.clone, body=%wide.region_1.3_spmd.clone.sunk | while | flops 1581772800 | bytes 8294561 | solution.py:44
  52.7 0.6 iota_compare_fusion.2
  53.3 5.9 %bitcast_add_fusion.2 = f32[8,120,800]{1,2,0:T(8,128)} fusion(f32[8,120,800]{1,2,0:T(8,128)} %get-tuple-element.216, pred[1024,800]{0,1:T(8,128)(4,1)S(1)} %iota_compare_fusion.2, bf16[8,1024]{1,0:T(8,128)(2,1)S(1)} %dynamic-slice_bitcast_fusion.2, pred[]{:T(512)S(6)} %compare.6, bf16[8192,120]{0,1:T(8,128)(2,1)} %get-tuple-element.228, ...), kind=kOutput, calls=%fused_computation.9.clone.1 | convolution fusion | flops 1580953600 | bytes 7430149 | tf_op jit(solution)/shard_map/while/body/eval_jaxpr/pi,vpm->vim/dot_general | solution.py:39
  59.2 0.6 iota_compare_fusion.2
  59.9 6.4 %bitcast_add_fusion.2 = f32[8,120,800]{1,2,0:T(8,128)} fusion(f32[8,120,800]{1,2,0:T(8,128)} %get-tuple-element.216, pred[1024,800]{0,1:T(8,128)(4,1)S(1)} %iota_compare_fusion.2, bf16[8,1024]{1,0:T(8,128)(2,1)S(1)} %dynamic-slice_bitcast_fusion.2, pred[]{:T(512)S(6)} %compare.6, bf16[8192,120]{0,1:T(8,128)(2,1)} %get-tuple-element.228, ...), kind=kOutput, calls=%fused_computation.9.clone.1 | convolution fusion | flops 1580953600 | bytes 7430149 | tf_op jit(solution)/shard_map/while/body/eval_jaxpr/pi,vpm->vim/dot_general | solution.py:39
  66.2 0.6 iota_compare_fusion.2
  66.9 6.4 %bitcast_add_fusion.2 = f32[8,120,800]{1,2,0:T(8,128)} fusion(f32[8,120,800]{1,2,0:T(8,128)} %get-tuple-element.216, pred[1024,800]{0,1:T(8,128)(4,1)S(1)} %iota_compare_fusion.2, bf16[8,1024]{1,0:T(8,128)(2,1)S(1)} %dynamic-slice_bitcast_fusion.2, pred[]{:T(512)S(6)} %compare.6, bf16[8192,120]{0,1:T(8,128)(2,1)} %get-tuple-element.228, ...), kind=kOutput, calls=%fused_computation.9.clone.1 | convolution fusion | flops 1580953600 | bytes 7430149 | tf_op jit(solution)/shard_map/while/body/eval_jaxpr/pi,vpm->vim/dot_general | solution.py:39
  73.2 0.6 iota_compare_fusion.2
  73.9 6.4 %bitcast_add_fusion.2 = f32[8,120,800]{1,2,0:T(8,128)} fusion(f32[8,120,800]{1,2,0:T(8,128)} %get-tuple-element.216, pred[1024,800]{0,1:T(8,128)(4,1)S(1)} %iota_compare_fusion.2, bf16[8,1024]{1,0:T(8,128)(2,1)S(1)} %dynamic-slice_bitcast_fusion.2, pred[]{:T(512)S(6)} %compare.6, bf16[8192,120]{0,1:T(8,128)(2,1)} %get-tuple-element.228, ...), kind=kOutput, calls=%fused_computation.9.clone.1 | convolution fusion | flops 1580953600 | bytes 7430149 | tf_op jit(solution)/shard_map/while/body/eval_jaxpr/pi,vpm->vim/dot_general | solution.py:39
  80.3 0.6 iota_compare_fusion.2
  80.9 6.4 %bitcast_add_fusion.2 = f32[8,120,800]{1,2,0:T(8,128)} fusion(f32[8,120,800]{1,2,0:T(8,128)} %get-tuple-element.216, pred[1024,800]{0,1:T(8,128)(4,1)S(1)} %iota_compare_fusion.2, bf16[8,1024]{1,0:T(8,128)(2,1)S(1)} %dynamic-slice_bitcast_fusion.2, pred[]{:T(512)S(6)} %compare.6, bf16[8192,120]{0,1:T(8,128)(2,1)} %get-tuple-element.228, ...), kind=kOutput, calls=%fused_computation.9.clone.1 | convolution fusion | flops 1580953600 | bytes 7430149 | tf_op jit(solution)/shard_map/while/body/eval_jaxpr/pi,vpm->vim/dot_general | solution.py:39
  87.3 0.6 iota_compare_fusion.2
  87.9 6.4 %bitcast_add_fusion.2 = f32[8,120,800]{1,2,0:T(8,128)} fusion(f32[8,120,800]{1,2,0:T(8,128)} %get-tuple-element.216, pred[1024,800]{0,1:T(8,128)(4,1)S(1)} %iota_compare_fusion.2, bf16[8,1024]{1,0:T(8,128)(2,1)S(1)} %dynamic-slice_bitcast_fusion.2, pred[]{:T(512)S(6)} %compare.6, bf16[8192,120]{0,1:T(8,128)(2,1)} %get-tuple-element.228, ...), kind=kOutput, calls=%fused_computation.9.clone.1 | convolution fusion | flops 1580953600 | bytes 7430149 | tf_op jit(solution)/shard_map/while/body/eval_jaxpr/pi,vpm->vim/dot_general | solution.py:39
  94.3 0.6 iota_compare_fusion.2
  94.9 6.4 %bitcast_add_fusion.2 = f32[8,120,800]{1,2,0:T(8,128)} fusion(f32[8,120,800]{1,2,0:T(8,128)} %get-tuple-element.216, pred[1024,800]{0,1:T(8,128)(4,1)S(1)} %iota_compare_fusion.2, bf16[8,1024]{1,0:T(8,128)(2,1)S(1)} %dynamic-slice_bitcast_fusion.2, pred[]{:T(512)S(6)} %compare.6, bf16[8192,120]{0,1:T(8,128)(2,1)} %get-tuple-element.228, ...), kind=kOutput, calls=%fused_computation.9.clone.1 | convolution fusion | flops 1580953600 | bytes 7430149 | tf_op jit(solution)/shard_map/while/body/eval_jaxpr/pi,vpm->vim/dot_general | solution.py:39
  101.3 0.6 iota_compare_fusion.2
  101.9 6.4 %bitcast_add_fusion.2 = f32[8,120,800]{1,2,0:T(8,128)} fusion(f32[8,120,800]{1,2,0:T(8,128)} %get-tuple-element.216, pred[1024,800]{0,1:T(8,128)(4,1)S(1)} %iota_compare_fusion.2, bf16[8,1024]{1,0:T(8,128)(2,1)S(1)} %dynamic-slice_bitcast_fusion.2, pred[]{:T(512)S(6)} %compare.6, bf16[8192,120]{0,1:T(8,128)(2,1)} %get-tuple-element.228, ...), kind=kOutput, calls=%fused_computation.9.clone.1 | convolution fusion | flops 1580953600 | bytes 7430149 | tf_op jit(solution)/shard_map/while/body/eval_jaxpr/pi,vpm->vim/dot_general | solution.py:39
  108.3 0.0 copy-start.3
  108.3 0.0 reduce-scatter.2.cloned.1.call-update
  108.3 0.6 copy-done.3
  109.0 0.0 copy-done
  109.0 1.6 gather_fusion
  110.6 0.0 copy-start.2
  110.6 2.4 convert_select_fusion
  113.0 0.0 copy-done.2
  113.0 0.1 copy.16
  113.1 133.3 %all-reduce.1 = bf16[256,3072]{1,0:T(8,128)(2,1)S(1)} all-reduce(f32[256,3072]{1,0:T(8,128)} %convert_select_fusion), channel_id=1, replica_groups=mesh['row'=32,'col'=8] {'row','col'}, use_global_device_ids=true, to_apply=%region_0.1 | all-reduce | flops 786432 | bytes 4718592 | tf_op jit(solution)/shard_map/psum | solution.py:57
  246.4 0.6 fusion.18
  247.0 0.8 copy.19
  247.7 0.0 reduce-scatter.2.cloned.1.call-done
  (25 shorter events, 0.2 us)
Async XLA Ops:
  7.2 101.8 %copy-start = (bf16[128,3072]{1,0:T(8,128)(2,1)S(1)}, bf16[128,3072]{1,0:T(8,128)(2,1)}, u32[]{:S(2)}) copy-start(bf16[128,3072]{1,0:T(8,128)(2,1)} %param.12) | copy-start | bytes 2359300
  7.2 14.2 %copy-start.1 = (bf16[800,120]{1,0:T(8,128)(2,1)S(1)}, bf16[800,120]{1,0:T(8,128)(2,1)}, u32[]{:S(2)}) copy-start(bf16[800,120]{1,0:T(8,128)(2,1)} %param.15) | copy-start | bytes 576004
  8.9 43.8 %all-to-all-start = ((bf16[128,32,8]{0,2,1:T(8,128)(2,1)}), bf16[128,32,8]{0,2,1:T(8,128)(2,1)S(1)}, u32[]{:S(2)}, u32[]{:S(2)}) async-start(bf16[128,32,8]{0,2,1:T(8,128)(2,1)} %bitcast.4), calls=%async_computation | async-start | bytes 131072 | tf_op jit(solution)/shard_map/all_to_all | solution.py:64
  19.3 228.5 %reduce-scatter.2.cloned.1.call-start = ((), (), s32[]{:S(2)}) async-start(), calls=%async_computation.2 | async-start | bytes 3686400 | tf_op jit(solution)/shard_map/reduce_scatter | solution.py:68
  108.3 0.7 copy-start.3
  110.6 2.4 copy-start.2
Sparse Core Ops, SparseCore 0:
  108.4 78.8 reduce-scatter.1
where the time goes:
time: 255 us
  blocking collectives  133 us (52%)
  matrix products  51.2 us (20%)
  local copies, waits for them, and re-layouts  32.1 us (13%)
  between operations  14.2 us (6%)
  other arithmetic  13.1 us (5%)
  starting transfers between devices  10.5 us (4%)
    psum x1, blocking collectives, per_device(): pivot_rows = lax.psum(contribution, ('row', 'col')).astype(jnp.bfloat16)  133 us
    dot_general x8, matrix products, one_block(): jnp.einsum('pi,vpm->vim', coeff_block, spread, preferred_element_type=jnp...  50.6 us
    gather x1, local copies, waits for them, and re-layouts, half_transform(): jnp.take(occupied, second_ao, axis=0)  12.1 us
    gather x1, local copies, waits for them, and re-layouts, half_transform(): occ_first = jnp.take(occupied, first_ao, axis=0)  12.1 us
    all_to_all x1, starting transfers between devices, per_device(): lax.all_to_all(grouped, 'row', split_axis=1, concat_axis=0, tiled=True)  10.4 us
    unnamed x12, local copies, waits for them, and re-layouts  6.15 us
  transfers between devices with their start and end apart: 2, of which 0 were waited for; matrix products, arithmetic and copies ran while one was open for 15% of the time, Pallas kernels for 0%

commit v1 on v0

--- a/solution.py
+++ b/solution.py
@@ -2,6 +2,13 @@
 import jax.numpy as jnp
 from jax import lax
 from jax.sharding import PartitionSpec as P
+from jax.lax import psum
+
+
+def shape_the_record(my_tile):
+    for to_i in ("col", "row"):
+        my_tile = psum(my_tile, to_i)
+    return my_tile
 
 
 def half_transform(received, pair_ids, occupied):
@@ -54,7 +61,7 @@
     owned = owner == own_index
     picked = jnp.take(prior, local_rows, axis=0).astype(jnp.float32)
     contribution = jnp.where(owned[:, None], picked, jnp.zeros_like(picked))
-    pivot_rows = lax.psum(contribution, ("row", "col")).astype(jnp.bfloat16)
+    pivot_rows = shape_the_record(contribution).astype(jnp.bfloat16)
     updated = panel - lax.dot_general(
         prior, pivot_rows, (((1,), (1,)), ((), ())), preferred_element_type=jnp.float32
     )

time: 255 us -> 368 us (1.44); the launches traced: 255 us -> 364 us
  waiting for transfers between devices: 0.02 us -> 59.3 us
  blocking collectives: 133 us -> 182 us
    psum x0 -> x1, waiting for transfers between devices: none -> 59.3 us  [shape_the_record(): my_tile = psum(my_tile, to_i)]
    psum x1, blocking collectives: 133 us -> 182 us  [shape_the_record(): my_tile = psum(my_tile, to_i)]
  transfers between devices with their start and end apart: 2 -> 3, of which waited for: 0 -> 1; matrix products, arithmetic and copies ran while one was open for 15% -> 26% of each run, Pallas kernels for 0% -> 0%
where the time goes in v1:
time: 368 us; the launch traced here: 364 us
  blocking collectives  182 us (49%)
  waiting for transfers between devices  59.3 us (16%)
  matrix products  51.4 us (14%)
  local copies, waits for them, and re-layouts  32.2 us (9%)
  between operations  14.2 us (4%)
  other arithmetic  13.9 us (4%)
  starting transfers between devices  10.5 us (3%)
    psum x1, blocking collectives, shape_the_record(): my_tile = psum(my_tile, to_i)  182 us
    psum x1, waiting for transfers between devices, shape_the_record(): my_tile = psum(my_tile, to_i)  59.3 us
    dot_general x8, matrix products, one_block(): jnp.einsum('pi,vpm->vim', coeff_block, spread, preferred_element_type=jnp...  50.9 us
    gather x1, local copies, waits for them, and re-layouts, half_transform(): jnp.take(occupied, second_ao, axis=0)  12.1 us
    gather x1, local copies, waits for them, and re-layouts, half_transform(): occ_first = jnp.take(occupied, first_ao, axis=0)  12.1 us
    all_to_all x1, starting transfers between devices, per_device(): lax.all_to_all(grouped, 'row', split_axis=1, concat_axis=0, tiled=True)  10.4 us
  transfers between devices with their start and end apart: 3, of which 1 were waited for; matrix products, arithmetic and copies ran while one was open for 26% of the time, Pallas kernels for 0%

profile of v1, /device:TPU:32, one launch (start us, length us, event | category | flops | bytes accessed | tf_op | source)
XLA Modules:
  0.0 363.6 jit_solution(9890308107096889617)
XLA Ops:
  7.2 0.0 copy-start
  7.2 1.6 copy.17
  8.8 10.4 %all-to-all-start = ((bf16[128,32,8]{0,2,1:T(8,128)(2,1)}), bf16[128,32,8]{0,2,1:T(8,128)(2,1)S(1)}, u32[]{:S(2)}, u32[]{:S(2)}) async-start(bf16[128,32,8]{0,2,1:T(8,128)(2,1)} %bitcast.4), calls=%async_computation | async-start | bytes 131072 | tf_op jit(solution)/shard_map/all_to_all | solution.py:71
  19.2 0.0 all-reduce.3.cloned.1.call-start
  19.3 0.7 compare_and_fusion.2
  20.0 0.0 copy-done
  20.0 1.6 gather_fusion
  21.6 0.0 copy-start.1
  21.6 2.4 convert_select_fusion
  24.0 0.0 all-reduce.3.cloned.1.call-update
  24.1 0.0 reduce-scatter.2.cloned.1.call-start
  24.1 1.0 broadcast_remainder_fusion
  25.1 1.0 compare_reduce_fusion
  26.2 0.0 copy-done.1
  26.2 12.1 %gather_fusion.2 = bf16[4096,120]{1,0:T(8,128)(2,1)S(1)} fusion(bf16[800,120]{1,0:T(8,128)(2,1)S(1)} %copy-done.1, s32[4096]{0:T(1024)S(1)} %get-tuple-element.172), kind=kCustom, calls=%fused_computation.1.clone | custom fusion | bytes 1982464 | tf_op jit(solution)/shard_map/jit(_take)/gather | solution.py:23
  38.3 12.1 %gather_fusion.1 = bf16[4096,120]{1,0:T(8,128)(2,1)S(1)} fusion(bf16[800,120]{1,0:T(8,128)(2,1)S(1)} %copy-done.1, s32[4096]{0:T(1024)S(1)} %fusion.21), kind=kCustom, calls=%fused_computation.clone | custom fusion | bytes 1982464 | tf_op jit(solution)/shard_map/jit(_take)/gather | solution.py:21
  50.5 2.1 broadcast_select_fusion
  52.6 1.4 select_select_fusion
  54.0 0.4 pad_maximum_fusion
  54.4 2.9 copy.18
  57.3 0.0 all-to-all-done
  57.4 55.9 %while.14 = (s32[]{:T(128)}, f32[8,120,800]{1,2,0:T(8,128)}, s32[8192]{0:T(1024)S(1)}, bf16[8192,8]{0,1:T(8,128)(2,1)S(1)}, bf16[8192,120]{0,1:T(8,128)(2,1)}, /*index=5*/s32[]{:T(128)}, s32[]{:T(128)}, s32[]{:T(128)}, s32[]{:T(128)}) while((s32[]{:T(128)}, f32[8,120,800]{1,2,0:T(8,128)}, s32[8192]{0:T(1024)S(1)}, ...), condition=%wide.region_3.5_spmd.clone, body=%wide.region_2.4_spmd.clone.sunk | while | flops 1581772800 | bytes 8294561 | solution.py:51
  57.4 0.6 iota_compare_fusion.2
  58.0 5.9 %bitcast_add_fusion.2 = f32[8,120,800]{1,2,0:T(8,128)} fusion(f32[8,120,800]{1,2,0:T(8,128)} %get-tuple-element.216, pred[1024,800]{0,1:T(8,128)(4,1)S(1)} %iota_compare_fusion.2, bf16[8,1024]{1,0:T(8,128)(2,1)S(1)} %dynamic-slice_bitcast_fusion.2, pred[]{:T(512)S(6)} %compare.6, bf16[8192,120]{0,1:T(8,128)(2,1)} %get-tuple-element.228, ...), kind=kOutput, calls=%fused_computation.9.clone.1 | convolution fusion | flops 1580953600 | bytes 7430149 | tf_op jit(solution)/shard_map/while/body/eval_jaxpr/pi,vpm->vim/dot_general | solution.py:46
  64.0 0.6 iota_compare_fusion.2
  64.6 6.4 %bitcast_add_fusion.2 = f32[8,120,800]{1,2,0:T(8,128)} fusion(f32[8,120,800]{1,2,0:T(8,128)} %get-tuple-element.216, pred[1024,800]{0,1:T(8,128)(4,1)S(1)} %iota_compare_fusion.2, bf16[8,1024]{1,0:T(8,128)(2,1)S(1)} %dynamic-slice_bitcast_fusion.2, pred[]{:T(512)S(6)} %compare.6, bf16[8192,120]{0,1:T(8,128)(2,1)} %get-tuple-element.228, ...), kind=kOutput, calls=%fused_computation.9.clone.1 | convolution fusion | flops 1580953600 | bytes 7430149 | tf_op jit(solution)/shard_map/while/body/eval_jaxpr/pi,vpm->vim/dot_general | solution.py:46
  71.0 0.6 iota_compare_fusion.2
  71.6 6.4 %bitcast_add_fusion.2 = f32[8,120,800]{1,2,0:T(8,128)} fusion(f32[8,120,800]{1,2,0:T(8,128)} %get-tuple-element.216, pred[1024,800]{0,1:T(8,128)(4,1)S(1)} %iota_compare_fusion.2, bf16[8,1024]{1,0:T(8,128)(2,1)S(1)} %dynamic-slice_bitcast_fusion.2, pred[]{:T(512)S(6)} %compare.6, bf16[8192,120]{0,1:T(8,128)(2,1)} %get-tuple-element.228, ...), kind=kOutput, calls=%fused_computation.9.clone.1 | convolution fusion | flops 1580953600 | bytes 7430149 | tf_op jit(solution)/shard_map/while/body/eval_jaxpr/pi,vpm->vim/dot_general | solution.py:46
  78.1 0.6 iota_compare_fusion.2
  78.7 6.4 %bitcast_add_fusion.2 = f32[8,120,800]{1,2,0:T(8,128)} fusion(f32[8,120,800]{1,2,0:T(8,128)} %get-tuple-element.216, pred[1024,800]{0,1:T(8,128)(4,1)S(1)} %iota_compare_fusion.2, bf16[8,1024]{1,0:T(8,128)(2,1)S(1)} %dynamic-slice_bitcast_fusion.2, pred[]{:T(512)S(6)} %compare.6, bf16[8192,120]{0,1:T(8,128)(2,1)} %get-tuple-element.228, ...), kind=kOutput, calls=%fused_computation.9.clone.1 | convolution fusion | flops 1580953600 | bytes 7430149 | tf_op jit(solution)/shard_map/while/body/eval_jaxpr/pi,vpm->vim/dot_general | solution.py:46
  85.1 0.6 iota_compare_fusion.2
  85.7 6.4 %bitcast_add_fusion.2 = f32[8,120,800]{1,2,0:T(8,128)} fusion(f32[8,120,800]{1,2,0:T(8,128)} %get-tuple-element.216, pred[1024,800]{0,1:T(8,128)(4,1)S(1)} %iota_compare_fusion.2, bf16[8,1024]{1,0:T(8,128)(2,1)S(1)} %dynamic-slice_bitcast_fusion.2, pred[]{:T(512)S(6)} %compare.6, bf16[8192,120]{0,1:T(8,128)(2,1)} %get-tuple-element.228, ...), kind=kOutput, calls=%fused_computation.9.clone.1 | convolution fusion | flops 1580953600 | bytes 7430149 | tf_op jit(solution)/shard_map/while/body/eval_jaxpr/pi,vpm->vim/dot_general | solution.py:46
  92.1 0.6 iota_compare_fusion.2
  92.8 6.4 %bitcast_add_fusion.2 = f32[8,120,800]{1,2,0:T(8,128)} fusion(f32[8,120,800]{1,2,0:T(8,128)} %get-tuple-element.216, pred[1024,800]{0,1:T(8,128)(4,1)S(1)} %iota_compare_fusion.2, bf16[8,1024]{1,0:T(8,128)(2,1)S(1)} %dynamic-slice_bitcast_fusion.2, pred[]{:T(512)S(6)} %compare.6, bf16[8192,120]{0,1:T(8,128)(2,1)} %get-tuple-element.228, ...), kind=kOutput, calls=%fused_computation.9.clone.1 | convolution fusion | flops 1580953600 | bytes 7430149 | tf_op jit(solution)/shard_map/while/body/eval_jaxpr/pi,vpm->vim/dot_general | solution.py:46
  99.2 0.6 iota_compare_fusion.2
  99.8 6.4 %bitcast_add_fusion.2 = f32[8,120,800]{1,2,0:T(8,128)} fusion(f32[8,120,800]{1,2,0:T(8,128)} %get-tuple-element.216, pred[1024,800]{0,1:T(8,128)(4,1)S(1)} %iota_compare_fusion.2, bf16[8,1024]{1,0:T(8,128)(2,1)S(1)} %dynamic-slice_bitcast_fusion.2, pred[]{:T(512)S(6)} %compare.6, bf16[8192,120]{0,1:T(8,128)(2,1)} %get-tuple-element.228, ...), kind=kOutput, calls=%fused_computation.9.clone.1 | convolution fusion | flops 1580953600 | bytes 7430149 | tf_op jit(solution)/shard_map/while/body/eval_jaxpr/pi,vpm->vim/dot_general | solution.py:46
  106.2 0.6 iota_compare_fusion.2
  106.9 6.4 %bitcast_add_fusion.2 = f32[8,120,800]{1,2,0:T(8,128)} fusion(f32[8,120,800]{1,2,0:T(8,128)} %get-tuple-element.216, pred[1024,800]{0,1:T(8,128)(4,1)S(1)} %iota_compare_fusion.2, bf16[8,1024]{1,0:T(8,128)(2,1)S(1)} %dynamic-slice_bitcast_fusion.2, pred[]{:T(512)S(6)} %compare.6, bf16[8192,120]{0,1:T(8,128)(2,1)} %get-tuple-element.228, ...), kind=kOutput, calls=%fused_computation.9.clone.1 | convolution fusion | flops 1580953600 | bytes 7430149 | tf_op jit(solution)/shard_map/while/body/eval_jaxpr/pi,vpm->vim/dot_general | solution.py:46
  113.3 0.0 copy-start.2
  113.3 0.0 reduce-scatter.2.cloned.1.call-update
  113.3 0.9 copy-done.2
  114.2 0.1 copy.16
  114.3 59.3 %all-reduce.3.cloned.1.call-done = f32[256,3072]{1,0:T(8,128)} async-done(((f32[256,3072]{1,0:T(8,128)}), f32[256,3072]{1,0:T(8,128)}) %all-reduce.3.cloned.1.call-update) | async-done | bytes 3145744 | tf_op jit(solution)/shard_map/psum | solution.py:10
  173.5 181.9 %all-reduce.4 = bf16[256,3072]{1,0:T(8,128)(2,1)S(1)} all-reduce(f32[256,3072]{1,0:T(8,128)} %all-reduce.3.cloned.1.call-done), channel_id=1, replica_groups=mesh['row'=32,'col'=8] {'row'}, use_global_device_ids=true, to_apply=%region_1.2 | all-reduce | flops 786432 | bytes 4718592 | tf_op jit(solution)/shard_map/psum | solution.py:10
  355.5 0.6 fusion.18
  356.0 0.8 copy.19
  356.8 0.0 reduce-scatter.2.cloned.1.call-done
  (24 shorter events, 0.2 us)
Async XLA Ops:
  7.2 12.9 %copy-start = (bf16[128,3072]{1,0:T(8,128)(2,1)S(1)}, bf16[128,3072]{1,0:T(8,128)(2,1)}, u32[]{:S(2)}) copy-start(bf16[128,3072]{1,0:T(8,128)(2,1)} %param.12) | copy-start | bytes 2359300
  8.8 48.5 %all-to-all-start = ((bf16[128,32,8]{0,2,1:T(8,128)(2,1)}), bf16[128,32,8]{0,2,1:T(8,128)(2,1)S(1)}, u32[]{:S(2)}, u32[]{:S(2)}) async-start(bf16[128,32,8]{0,2,1:T(8,128)(2,1)} %bitcast.4), calls=%async_computation | async-start | bytes 131072 | tf_op jit(solution)/shard_map/all_to_all | solution.py:71
  19.2 154.3 %all-reduce.3.cloned.1.call-start = ((), (), s32[]{:S(2)}) async-start(), calls=%async_computation.2 | async-start | bytes 6291456 | tf_op jit(solution)/shard_map/psum | solution.py:10
  21.6 4.6 %copy-start.1 = (bf16[800,120]{1,0:T(8,128)(2,1)S(1)}, bf16[800,120]{1,0:T(8,128)(2,1)}, u32[]{:S(2)}) copy-start(bf16[800,120]{1,0:T(8,128)(2,1)} %param.15) | copy-start | bytes 576004
  24.1 332.7 %reduce-scatter.2.cloned.1.call-start = ((), (), s32[]{:S(2)}) async-start(), calls=%async_computation.3 | async-start | bytes 3686400 | tf_op jit(solution)/shard_map/reduce_scatter | solution.py:75
  113.3 0.9 copy-start.2
Sparse Core Ops, SparseCore 0:
  24.2 149.3 all-reduce.2
  176.7 106.9 reduce-scatter.1
